TPU v7x, 32 devices: a whole 2x2x4 slice. The times are simulated.
32 devices in a mesh: row: 4 (over z), col: 8 (over y, x, core).
Axes of the slice: x: 2, y: 2, z: 4, core: 2. Of those that a mesh axis runs over, the one named last changes fastest.
Arguments:
- front_matrix: bfloat16 [32768, 32768], P('row', 'col'), may hold values from -0.03125 to 0.03125
- right_random: bfloat16 [32768, 128], P(('col', 'row')), may hold values from -32 to 32
- left_random: bfloat16 [32768, 128], P(('row', 'col')), may hold values from -32 to 32
- row_basis: bfloat16 [32768, 384], P('row'), may hold values from -1 to 1, as said below
- column_basis: bfloat16 [32768, 384], P('col'), may hold values from -1 to 1, as said below
Outputs:
- row_samples: float32 [128, 32768], P('col', 'row')
- column_samples: float32 [128, 32768], P('row', 'col')
- row_spread: float32 [64], P('row')
- column_spread: float32 [64], P('col')
Inputs may be any that keep to these rules, and one draw needn't show every extreme that they name: Within each leaf node's 512 rows, the columns of row_basis are orthonormal up to their rounding to bfloat16. Within each leaf node's 512 rows, the columns of column_basis are orthonormal up to their rounding to bfloat16.
All inputs are finite; a program needn't handle non-finite values.
Results may differ from a plain program's by a relative error of at most 0.0003.
Values may be sent and summed in bfloat16 or wider, within the bound.
No kernel may reach another device: no remote copies, remote signals or barrier semaphores. Data moves between devices by JAX's collectives and lax.ppermute only.
A program may use at most 128 MiB of HBM per device.

v0:
```python
import jax
import jax.numpy as jnp
from jax import lax
from jax.sharding import PartitionSpec as P

SAMPLES = 128
EARLIER = 384
NODE = 512


def project_out(samples, basis):
    count = samples.shape[0]
    nodes = basis.shape[0] // NODE
    shaped = samples.reshape(count, nodes, NODE)
    stacked = basis.astype(jnp.float32).reshape(nodes, NODE, EARLIER)
    coeffs = jnp.einsum("knr,nre->kne", shaped, stacked, precision=lax.Precision.HIGHEST)
    correction = jnp.einsum("kne,nre->knr", coeffs, stacked, precision=lax.Precision.HIGHEST)
    cleaned = shaped - correction
    squares = jnp.sum(cleaned * cleaned, axis=(0, 2))
    return (cleaned.reshape(count, nodes * NODE), squares)


def shards(front_matrix, right_random, left_random, row_basis, column_basis):
    row_partial = jnp.einsum(
        "jc,ij->ci",
        lax.all_gather(right_random, "row", axis=0, tiled=True),
        front_matrix,
        preferred_element_type=jnp.float32,
    )
    column_partial = jnp.einsum(
        "ic,ij->cj",
        lax.all_gather(left_random, "col", axis=0, tiled=True),
        front_matrix,
        preferred_element_type=jnp.float32,
    )
    row_mine = lax.psum_scatter(row_partial, "col", scatter_dimension=0, tiled=True)
    column_mine = lax.psum_scatter(column_partial, "row", scatter_dimension=0, tiled=True)
    row_samples, row_partial_sq = project_out(row_mine, row_basis)
    column_samples, column_partial_sq = project_out(column_mine, column_basis)
    row_total_sq = lax.psum(row_partial_sq, "col")
    column_total_sq = lax.psum(column_partial_sq, "row")
    row_spread = jnp.sqrt(row_total_sq / (SAMPLES * NODE))
    column_spread = jnp.sqrt(column_total_sq / (SAMPLES * NODE))
    return (row_samples, column_samples, row_spread, column_spread)


def solution(mesh):
    in_specs = (
        P("row", "col"),
        P(("col", "row"), None),
        P(("row", "col"), None),
        P("row", None),
        P("col", None),
    )
    out_specs = (P("col", "row"), P("row", "col"), P("row"), P("col"))
    return jax.shard_map(shards, mesh=mesh, in_specs=in_specs, out_specs=out_specs, check_vma=False)
```

profile of v0, /device:TPU:0, one launch (start us, length us, event | category | flops | bytes accessed | tf_op | source)
XLA Modules:
  0.0 207.1 jit_solution(11374009316376437406)
XLA Ops:
  7.2 0.0 copy-start
  7.2 0.0 all-gather.3.cloned.1.call-start
  7.2 0.7 all-gather.3.cloned.1.call-update
  7.9 0.0 all-gather.5.cloned.1.call-start
  8.0 0.7 all-gather.5.cloned.1.call-update
  8.7 0.0 reduce-scatter.3.cloned.1.call-start
  8.7 31.6 %all-gather.3.cloned.1.call-done = bf16[4096,128]{1,0:T(8,128)(2,1)} async-done(((bf16[1024,128]{1,0:T(8,128)(2,1)}), bf16[4096,128]{1,0:T(8,128)(2,1)}) %all-gather.3.cloned.1.call-update) | async-done | bytes 1048592 | tf_op jit(solution)/shard_map/all_gather | solution.py:26
  40.3 29.5 %fusion.6 = f32[128,8192]{1,0:T(8,128)} fusion(bf16[4096,128]{1,0:T(8,128)(2,1)} %all-gather.3.cloned.1.call-done, bf16[8192,4096]{1,0:T(8,128)(2,1)} %param.5), kind=kOutput, calls=%fused_computation.14 | convolution fusion | flops 8589934592 | bytes 72351744 | tf_op jit(solution)/shard_map/jc,ij->ci/dot_general | solution.py:24
  69.8 0.0 reduce-scatter.3.cloned.1.call-update
  69.8 0.2 reduce-scatter.5.cloned.1.call-start
  70.1 0.0 all-gather.5.cloned.1.call-done
  70.1 27.7 %fusion.7 = f32[128,4096]{1,0:T(8,128)} fusion(bf16[8192,128]{1,0:T(8,128)(2,1)} %all-gather.5.cloned.1.call-done, bf16[8192,4096]{1,0:T(8,128)(2,1)} %param.5), kind=kOutput, calls=%fused_computation.15 | convolution fusion | flops 8589934592 | bytes 71303168 | tf_op jit(solution)/shard_map/ic,ij->cj/dot_general | solution.py:30
  97.7 0.0 reduce-scatter.5.cloned.1.call-update
  97.8 26.1 %reduce-scatter.3.cloned.1.call-done = f32[16,8192]{1,0:T(8,128)} async-done(((f32[128,8192]{1,0:T(8,128)}), f32[16,8192]{1,0:T(8,128)}) %reduce-scatter.3.cloned.1.call-update) | async-done | bytes 524304 | tf_op jit(solution)/shard_map/reduce_scatter | solution.py:36
  123.9 0.0 copy-start.2
  123.9 5.6 %convolution_bitcast_fusion.3 = f32[16,16,384]{2,0,1:T(8,128)S(1)} fusion(bf16[16,512,384]{2,1,0:T(8,128)(2,1)} %bitcast.40, f32[2,16,8,512]{3,2,1,0:T(8,128)} %bitcast.45), kind=kOutput, calls=%fused_computation.5 | convolution fusion | flops 603979776 | bytes 7208960 | tf_op jit(solution)/shard_map/knr,nre->kne/dot_general | solution.py:16
  129.5 0.0 copy-done.2
  129.5 7.2 %multiply_reduce_fusion.1 = (f32[16]{0:T(128)S(1)}, f32[16,16,512]{2,0,1:T(8,128)S(1)}) fusion(f32[16,16,384]{2,0,1:T(8,128)S(1)} %convolution_bitcast_fusion.3, bf16[16,512,384]{2,1,0:T(8,128)(2,1)} %bitcast.41, f32[2,16,8,512]{3,2,1,0:T(8,128)S(1)} %bitcast.46), kind=kOutput, calls=%fused_computation.9 | convolution fusion | flops 604372992 | bytes 7733312 | tf_op jit(solution)/shard_map/kne,nre->knr/dot_general | solution.py:17
  136.7 0.8 copy.17
  137.5 32.2 %reduce-scatter.5.cloned.1.call-done = f32[32,4096]{1,0:T(8,128)} async-done(((f32[128,4096]{1,0:T(8,128)}), f32[32,4096]{1,0:T(8,128)}) %reduce-scatter.5.cloned.1.call-update) | async-done | bytes 524304 | tf_op jit(solution)/shard_map/reduce_scatter | solution.py:37
  169.7 0.0 copy-done
  169.7 0.0 copy-start.1
  169.7 2.6 %convolution_bitcast_fusion.2 = f32[32,8,384]{2,0,1:T(8,128)S(1)} fusion(bf16[8,512,384]{2,1,0:T(8,128)(2,1)S(1)} %bitcast.38, f32[4,8,8,512]{3,2,1,0:T(8,128)} %bitcast.43), kind=kOutput, calls=%fused_computation.4 | convolution fusion | flops 603979776 | bytes 4063232 | tf_op jit(solution)/shard_map/knr,nre->kne/dot_general | solution.py:16
  172.3 0.0 copy-done.1
  172.4 3.0 %multiply_reduce_fusion = (f32[8]{0:T(128)S(1)}, f32[32,8,512]{2,0,1:T(8,128)S(1)}) fusion(f32[32,8,384]{2,0,1:T(8,128)S(1)} %convolution_bitcast_fusion.2, bf16[8,512,384]{2,1,0:T(8,128)(2,1)S(1)} %bitcast.39, f32[4,8,8,512]{3,2,1,0:T(8,128)S(1)} %bitcast.44), kind=kOutput, calls=%fused_computation.8 | convolution fusion | flops 604372992 | bytes 4587552 | tf_op jit(solution)/shard_map/kne,nre->knr/dot_general | solution.py:17
  175.4 0.8 copy.18
  176.2 13.2 %psum.14 = f32[16]{0:T(128)S(1)} all-reduce(f32[16]{0:T(128)S(1)} %get-tuple-element.4), channel_id=1, replica_groups=mesh['row'=4,'col'=8] {'col'}, use_global_device_ids=true, to_apply=%region_3.0 | all-reduce | flops 16 | bytes 128 | tf_op jit(solution)/shard_map/psum | solution.py:40
  189.4 0.5 multiply_sqrt_fusion.1
  189.9 10.2 %psum.15 = f32[8]{0:T(128)S(1)} all-reduce(f32[8]{0:T(128)S(1)} %get-tuple-element.6), channel_id=1, replica_groups=mesh['row'=4,'col'=8] {'row'}, use_global_device_ids=true, to_apply=%region_5.0 | all-reduce | flops 8 | bytes 64 | tf_op jit(solution)/shard_map/psum | solution.py:41
  200.1 0.5 multiply_sqrt_fusion
Async XLA Ops:
  7.2 162.6 %copy-start = (bf16[4096,384]{1,0:T(8,128)(2,1)S(1)}, bf16[4096,384]{1,0:T(8,128)(2,1)}, u32[]{:S(2)}) copy-start(bf16[4096,384]{1,0:T(8,128)(2,1)} %param.9) | copy-start | bytes 9437188
  7.2 33.1 %all-gather.3.cloned.1.call-start = ((), (), s32[]{:S(2)}) async-start(), calls=%async_computation.2 | async-start | bytes 1310720 | tf_op jit(solution)/shard_map/all_gather | solution.py:26
  7.9 62.2 %all-gather.5.cloned.1.call-start = ((), (), s32[]{:S(2)}) async-start(), calls=%async_computation.4 | async-start | bytes 2359296 | tf_op jit(solution)/shard_map/all_gather | solution.py:32
  8.7 115.2 %reduce-scatter.3.cloned.1.call-start = ((), (), s32[]{:S(2)}) async-start(), calls=%async_computation.3 | async-start | bytes 4718592 | tf_op jit(solution)/shard_map/reduce_scatter | solution.py:36
  69.8 99.9 %reduce-scatter.5.cloned.1.call-start = ((), (), s32[]{:S(2)}) async-start(), calls=%async_computation.5 | async-start | bytes 2621440 | tf_op jit(solution)/shard_map/reduce_scatter | solution.py:37
  123.9 5.6 %copy-start.2 = (f32[16,8192]{1,0:T(8,128)S(1)}, f32[16,8192]{1,0:T(8,128)}, u32[]{:S(2)}) copy-start(f32[16,8192]{1,0:T(8,128)} %reduce-scatter.3.cloned.1.call-done) | copy-start | bytes 1572868
  169.7 2.6 %copy-start.1 = (f32[32,4096]{1,0:T(8,128)S(1)}, f32[32,4096]{1,0:T(8,128)}, u32[]{:S(2)}) copy-start(f32[32,4096]{1,0:T(8,128)} %reduce-scatter.5.cloned.1.call-done) | copy-start | bytes 1572868
Sparse Core Ops, SparseCore 0:
  9.6 30.6 all-gather.2
  42.2 27.1 all-gather.4
  72.7 51.1 reduce-scatter.2
  126.1 43.6 reduce-scatter.4
where the time goes:
time: 207 us
  waiting for transfers between devices  91.3 us (44%)
  matrix products  75.6 us (37%)
  blocking collectives  23.4 us (11%)
  between operations  13.8 us (7%)
    reduce_scatter x1, waiting for transfers between devices, shards(): lax.psum_scatter(column_partial, 'row', scatter_dimension=0, tiled=True)  32.2 us
    all_gather x1, waiting for transfers between devices, shards(): lax.all_gather(right_random, 'row', axis=0, tiled=True)  31.6 us
    dot_general x1, matrix products, shards(): jnp.einsum('jc,ij->ci', lax.all_gather(right_random, 'row', axis=0, tiled...  29.5 us
    dot_general x1, matrix products, shards(): jnp.einsum('ic,ij->cj', lax.all_gather(left_random, 'col', axis=0, tiled=...  27.7 us
    reduce_scatter x1, waiting for transfers between devices, shards(): lax.psum_scatter(row_partial, 'col', scatter_dimension=0, tiled=True)  26.1 us
    psum x1, blocking collectives, shards(): row_total_sq = lax.psum(row_partial_sq, 'col')  13.2 us
    dot_general x2, matrix products, project_out(): jnp.einsum('kne,nre->knr', coeffs, stacked, precision=lax.Precision.HIGHEST)  10.2 us
    psum x1, blocking collectives, shards(): column_total_sq = lax.psum(column_partial_sq, 'row')  10.2 us
  transfers between devices with their start and end apart: 4, of which 3 were waited for; matrix products, arithmetic and copies ran while one was open for 34% of the time, Pallas kernels for 0%

commit v1 on v0

--- a/solution.py
+++ b/solution.py
@@ -21,12 +21,22 @@
 
 
 def shards(front_matrix, right_random, left_random, row_basis, column_basis):
-    row_partial = jnp.einsum(
-        "jc,ij->ci",
-        lax.all_gather(right_random, "row", axis=0, tiled=True),
-        front_matrix,
-        preferred_element_type=jnp.float32,
-    )
+    count_2, index, rows = (lax.axis_size("row"), lax.axis_index("row"), right_random.shape[0])
+    upward = [(i, (i + 1) % count_2) for i in range(count_2)]
+    held, subtotal = (right_random, None)
+    for step in range(count_2):
+        arriving = lax.ppermute(held, "row", upward) if step < count_2 - 1 else None
+        absorb = jnp.einsum(
+            "jc,ij->ci",
+            held,
+            lax.dynamic_slice_in_dim(
+                front_matrix, (index - step) % count_2 * rows, held.shape[0], axis=1
+            ),
+            preferred_element_type=jnp.float32,
+        )
+        subtotal = absorb if subtotal is None else subtotal + absorb
+        held = arriving
+    row_partial = subtotal
     column_partial = jnp.einsum(
         "ic,ij->cj",
         lax.all_gather(left_random, "col", axis=0, tiled=True),

time: 207 us -> 182 us (0.88)
  waiting for transfers between devices: 91.3 us -> 29.7 us
  matrix products: 75.6 us -> 91.6 us
  local copies, waits for them, and re-layouts: 1.69 us -> 15.3 us
  starting transfers between devices: 0.34 us -> 6.71 us
    all_gather x1 -> x0, waiting for transfers between devices: 31.6 us -> none  [shards(): lax.all_gather(right_random, 'row', axis=0, tiled=True)]
    reduce_scatter x1 -> x0, waiting for transfers between devices: 26.1 us -> none  [shards(): lax.psum_scatter(row_partial, 'col', scatter_dimension=0, tiled=True)]
    reduce_scatter x1, waiting for transfers between devices: 32.2 us -> 6.49 us  [shards(): lax.psum_scatter(column_partial, 'row', scatter_dimension=0, tiled=True)]
    unnamed x4, waiting for transfers between devices: 1.41 us -> 23.2 us
    dot_general x1 -> x4, matrix products: 29.5 us -> 41.1 us  [shards(): jnp.einsum('jc,ij->ci', held, lax.dynamic_slice_in_dim(front_matrix, (ind...]
    unnamed x6 -> x8, local copies, waits for them, and re-layouts: 0.02 us -> 9.13 us
    ppermute x0 -> x3, starting transfers between devices: none -> 6.37 us  [shards(): arriving = lax.ppermute(held, 'row', upward) if step < count_2 - 1 else None]
    reshape x0 -> x1, local copies, waits for them, and re-layouts: none -> 3.5 us  [project_out(): shaped = samples.reshape(count, nodes, NODE)]
  transfers between devices with their start and end apart: 4 -> 6, of which waited for: 3 -> 2; matrix products, arithmetic and copies ran while one was open for 34% -> 56% of each run, Pallas kernels for 0% -> 0%
where the time goes in v1:
time: 182 us
  matrix products  91.6 us (50%)
  waiting for transfers between devices  29.7 us (16%)
  blocking collectives  23.7 us (13%)
  local copies, waits for them, and re-layouts  15.3 us (8%)
  between operations  13.8 us (8%)
  starting transfers between devices  6.71 us (4%)
    dot_general x4, matrix products, shards(): jnp.einsum('jc,ij->ci', held, lax.dynamic_slice_in_dim(front_matrix, (ind...  41.1 us
    dot_general x1, matrix products, shards(): jnp.einsum('ic,ij->cj', lax.all_gather(left_random, 'col', axis=0, tiled=...  28.4 us
    unnamed x4, waiting for transfers between devices  23.2 us
    psum x1, blocking collectives, shards(): row_total_sq = lax.psum(row_partial_sq, 'col')  13.6 us
    dot_general x2, matrix products, project_out(): jnp.einsum('kne,nre->knr', coeffs, stacked, precision=lax.Precision.HIGHEST)  11.6 us
    dot_general x2, matrix products, project_out(): jnp.einsum('knr,nre->kne', shaped, stacked, precision=lax.Precision.HIGHEST)  10.5 us
    psum x1, blocking collectives, shards(): column_total_sq = lax.psum(column_partial_sq, 'row')  10.1 us
    unnamed x8, local copies, waits for them, and re-layouts  9.13 us
  transfers between devices with their start and end apart: 6, of which 2 were waited for; matrix products, arithmetic and copies ran while one was open for 56% of the time, Pallas kernels for 0%

profile of v1, /device:TPU:0, one launch (start us, length us, event | category | flops | bytes accessed | tf_op | source)
XLA Modules:
  0.0 181.9 jit_solution(6840211523511487224)
XLA Ops:
  7.2 0.0 copy-start
  7.2 0.0 all-gather.2.cloned.1.call-start
  7.2 0.7 all-gather.2.cloned.1.call-update
  7.9 0.0 reduce-scatter.7.cloned.1.call-start
  8.0 3.1 %collective-permute-start = (bf16[1024,128]{1,0:T(8,128)(2,1)}, bf16[1024,128]{1,0:T(8,128)(2,1)S(1)}, u32[]{:S(2)}, u32[]{:S(2)}) collective-permute-start(bf16[1024,128]{1,0:T(8,128)(2,1)} %param.6), channel_id=1, source_target_pairs={{0,8},{8,16},{16,24},{24,0},{1,9},{9,17},{17,25},{25,1},{2,10},{10... | collective-permute-start | bytes 786440 | tf_op jit(solution)/shard_map/ppermute | solution.py:28
  11.1 12.2 %fusion.6 = f32[8192,128]{1,0:T(8,128)} fusion(bf16[1024,128]{1,0:T(8,128)(2,1)} %param.6, bf16[8192,4096]{1,0:T(8,128)(2,1)} %param.5, s32[]{:T(128)S(6)} %select_n.32), kind=kOutput, calls=%fused_computation.6 | convolution fusion | flops 2147483648 | bytes 21233668 | tf_op jit(solution)/shard_map/jc,ij->ci/dot_general | solution.py:29
  23.3 0.0 collective-permute-done
  23.3 1.6 collective-permute-start.1
  24.9 10.1 %fusion.8 = f32[8192,128]{1,0:T(8,128)S(1)} fusion(f32[8192,128]{1,0:T(8,128)} %fusion.6, bf16[1024,128]{1,0:T(8,128)(2,1)S(1)} %collective-permute-done, bf16[8192,4096]{1,0:T(8,128)(2,1)} %param.5, s32[]{:T(128)S(6)} %select_n.34), kind=kOutput, calls=%fused_computation.8 | convolution fusion | flops 2148532224 | bytes 25427972 | tf_op jit(solution)/shard_map/jc,ij->ci/dot_general | solution.py:29
  35.0 0.0 collective-permute-done.1
  35.0 1.7 collective-permute-start.2
  36.7 8.3 %fusion.11 = f32[8192,128]{1,0:T(8,128)S(1)} fusion(f32[8192,128]{1,0:T(8,128)S(1)} %fusion.8, bf16[1024,128]{1,0:T(8,128)(2,1)S(1)} %collective-permute-done.1, bf16[8192,4096]{1,0:T(8,128)(2,1)} %param.5, s32[]{:T(128)S(6)} %select_n.36), kind=kOutput, calls=%fused_computation.9 | convolution fusion | flops 2148532224 | bytes 25427972 | tf_op jit(solution)/shard_map/jc,ij->ci/dot_general | solution.py:29
  44.9 0.0 collective-permute-done.2
  45.0 10.5 %fusion.17 = f32[128,8192]{0,1:T(8,128)} fusion(f32[8192,128]{1,0:T(8,128)S(1)} %fusion.11, bf16[1024,128]{1,0:T(8,128)(2,1)S(1)} %collective-permute-done.2, bf16[8192,4096]{1,0:T(8,128)(2,1)} %param.5, s32[]{:T(128)S(6)} %select_n.38), kind=kOutput, calls=%fused_computation.11 | convolution fusion | flops 2148532224 | bytes 25427972 | tf_op jit(solution)/shard_map/jc,ij->ci/dot_general | solution.py:29
  55.5 5.6 %copy.29 = f32[128,8192]{1,0:T(8,128)} copy(f32[128,8192]{0,1:T(8,128)} %fusion.17) | data formatting | bytes 8388608
  61.1 0.0 reduce-scatter.7.cloned.1.call-update
  61.1 0.3 reduce-scatter.5.cloned.1.call-start
  61.4 0.0 all-gather.2.cloned.1.call-done
  61.4 28.4 %fusion.28 = f32[128,4096]{1,0:T(8,128)} fusion(bf16[8192,128]{1,0:T(8,128)(2,1)} %all-gather.2.cloned.1.call-done, bf16[8192,4096]{1,0:T(8,128)(2,1)} %param.5), kind=kOutput, calls=%fused_computation.28 | convolution fusion | flops 8589934592 | bytes 71303168 | tf_op jit(solution)/shard_map/ic,ij->cj/dot_general | solution.py:40
  89.8 0.0 reduce-scatter.5.cloned.1.call-update
  89.8 22.5 %reduce-scatter.7.cloned.1.call-done = f32[16,8192]{1,0:T(8,128)} async-done(((f32[128,8192]{1,0:T(8,128)}), f32[16,8192]{1,0:T(8,128)}) %reduce-scatter.7.cloned.1.call-update) | async-done | bytes 524304
  112.3 3.5 %copy.30 = f32[16,8192]{0,1:T(8,128)} copy(f32[16,8192]{1,0:T(8,128)} %reduce-scatter.7.cloned.1.call-done) | data formatting | bytes 1048576
  115.8 3.5 %copy.21 = f32[16,16,512]{2,0,1:T(8,128)} copy(f32[16,16,512]{0,2,1:T(8,128)} %bitcast.42) | data formatting | bytes 1048576 | tf_op jit(solution)/shard_map/reshape | solution.py:14
  119.3 0.0 copy-start.2
  119.3 7.9 %convolution_bitcast_fusion.3 = f32[16,16,384]{2,0,1:T(8,128)S(1)} fusion(f32[16,16,512]{0,2,1:T(8,128)} %bitcast.43, bf16[16,512,384]{2,1,0:T(8,128)(2,1)} %bitcast.44), kind=kOutput, calls=%fused_computation.17 | convolution fusion | flops 603979776 | bytes 7208960 | tf_op jit(solution)/shard_map/knr,nre->kne/dot_general | solution.py:16
  127.2 0.0 copy-done.2
  127.2 8.6 %multiply_reduce_fusion.1 = (f32[16]{0:T(128)S(1)}, f32[16,16,512]{2,0,1:T(8,128)}) fusion(f32[16,16,512]{2,0,1:T(8,128)S(1)} %copy-done.2, f32[16,16,384]{2,0,1:T(8,128)S(1)} %convolution_bitcast_fusion.3, bf16[16,512,384]{2,1,0:T(8,128)(2,1)} %bitcast.45), kind=kOutput, calls=%fused_computation.20 | convolution fusion | flops 604372992 | bytes 7733312 | tf_op jit(solution)/shard_map/kne,nre->knr/dot_general | solution.py:17
  135.8 13.6 %psum.14 = f32[16]{0:T(128)S(1)} all-reduce(f32[16]{0:T(128)S(1)} %get-tuple-element.4), channel_id=1, replica_groups=mesh['row'=4,'col'=8] {'col'}, use_global_device_ids=true, to_apply=%region_3.4 | all-reduce | flops 16 | bytes 128 | tf_op jit(solution)/shard_map/psum | solution.py:50
  149.4 1.9 %copy.32 = f32[16,2,8,512]{3,2,0,1:T(8,128)} copy(f32[16,2,8,512]{3,2,1,0:T(8,128)} %bitcast.49) | data formatting | bytes 1048576 | tf_op jit(solution)/shard_map/reshape | solution.py:20
  151.3 0.5 multiply_sqrt_fusion.1
  151.8 6.5 %reduce-scatter.5.cloned.1.call-done = f32[32,4096]{1,0:T(8,128)} async-done(((f32[128,4096]{1,0:T(8,128)}), f32[32,4096]{1,0:T(8,128)}) %reduce-scatter.5.cloned.1.call-update) | async-done | bytes 524304 | tf_op jit(solution)/shard_map/reduce_scatter | solution.py:47
  158.3 0.0 copy-start.1
  158.3 0.0 copy-done
  158.3 2.6 %convolution_bitcast_fusion.2 = f32[32,8,384]{2,0,1:T(8,128)S(1)} fusion(bf16[8,512,384]{2,1,0:T(8,128)(2,1)S(1)} %bitcast.40, f32[4,8,8,512]{3,2,1,0:T(8,128)} %bitcast.47), kind=kOutput, calls=%fused_computation.16 | convolution fusion | flops 603979776 | bytes 4063232 | tf_op jit(solution)/shard_map/knr,nre->kne/dot_general | solution.py:16
  160.9 0.0 copy-done.1
  160.9 3.0 %multiply_reduce_fusion = (f32[8]{0:T(128)S(1)}, f32[32,8,512]{2,0,1:T(8,128)S(1)}) fusion(f32[32,8,384]{2,0,1:T(8,128)S(1)} %convolution_bitcast_fusion.2, bf16[8,512,384]{2,1,0:T(8,128)(2,1)S(1)} %bitcast.41, f32[4,8,8,512]{3,2,1,0:T(8,128)S(1)} %bitcast.48), kind=kOutput, calls=%fused_computation.19 | convolution fusion | flops 604372992 | bytes 4587552 | tf_op jit(solution)/shard_map/kne,nre->knr/dot_general | solution.py:17
  163.9 0.8 copy.33
  164.7 10.1 %psum.15 = f32[8]{0:T(128)S(1)} all-reduce(f32[8]{0:T(128)S(1)} %get-tuple-element.6), channel_id=1, replica_groups=mesh['row'=4,'col'=8] {'row'}, use_global_device_ids=true, to_apply=%region_5.6 | all-reduce | flops 8 | bytes 64 | tf_op jit(solution)/shard_map/psum | solution.py:51
  174.8 0.5 multiply_sqrt_fusion
Async XLA Ops:
  7.2 151.1 %copy-start = (bf16[4096,384]{1,0:T(8,128)(2,1)S(1)}, bf16[4096,384]{1,0:T(8,128)(2,1)}, u32[]{:S(2)}) copy-start(bf16[4096,384]{1,0:T(8,128)(2,1)} %param.9) | copy-start | bytes 9437188
  7.2 54.2 %all-gather.2.cloned.1.call-start = ((), (), s32[]{:S(2)}) async-start(), calls=%async_computation.2 | async-start | bytes 2359296 | tf_op jit(solution)/shard_map/all_gather | solution.py:42
  7.9 104.4 %reduce-scatter.7.cloned.1.call-start = ((), (), s32[]{:S(2)}) async-start(), calls=%async_computation.4 | async-start | bytes 4718592
  8.0 15.3 %collective-permute-start = (bf16[1024,128]{1,0:T(8,128)(2,1)}, bf16[1024,128]{1,0:T(8,128)(2,1)S(1)}, u32[]{:S(2)}, u32[]{:S(2)}) collective-permute-start(bf16[1024,128]{1,0:T(8,128)(2,1)} %param.6), channel_id=1, source_target_pairs={{0,8},{8,16},{16,24},{24,0},{1,9},{9,17},{17,25},{25,1},{2,10},{10... | collective-permute-start | bytes 786440 | tf_op jit(solution)/shard_map/ppermute | solution.py:28
  23.3 11.7 %collective-permute-start.1 = (bf16[1024,128]{1,0:T(8,128)(2,1)S(1)}, bf16[1024,128]{1,0:T(8,128)(2,1)S(1)}, u32[]{:S(2)}, u32[]{:S(2)}) collective-permute-start(bf16[1024,128]{1,0:T(8,128)(2,1)S(1)} %collective-permute-done), channel_id=1, source_target_pairs={{0,8},{8,16},{16,24},{24,0},{1,9},{9,17},{17,25},{25,1},{2,10},{10... | collective-permute-start | bytes 786440 | tf_op jit(solution)/shard_map/ppermute | solution.py:28
  35.0 10.0 %collective-permute-start.2 = (bf16[1024,128]{1,0:T(8,128)(2,1)S(1)}, bf16[1024,128]{1,0:T(8,128)(2,1)S(1)}, u32[]{:S(2)}, u32[]{:S(2)}) collective-permute-start(bf16[1024,128]{1,0:T(8,128)(2,1)S(1)} %collective-permute-done.1), channel_id=1, source_target_pairs={{0,8},{8,16},{16,24},{24,0},{1,9},{9,17},{17,25},{25,1},{2,10},{10... | collective-permute-start | bytes 786440 | tf_op jit(solution)/shard_map/ppermute | solution.py:28
  61.1 97.1 %reduce-scatter.5.cloned.1.call-start = ((), (), s32[]{:S(2)}) async-start(), calls=%async_computation.3 | async-start | bytes 2621440 | tf_op jit(solution)/shard_map/reduce_scatter | solution.py:47
  119.3 7.9 %copy-start.2 = (f32[16,16,512]{2,0,1:T(8,128)S(1)}, f32[16,16,512]{2,0,1:T(8,128)}, u32[]{:S(2)}) copy-start(f32[16,16,512]{2,0,1:T(8,128)} %copy.21) | copy-start | bytes 1572868
  158.3 2.6 %copy-start.1 = (f32[32,4096]{1,0:T(8,128)S(1)}, f32[32,4096]{1,0:T(8,128)}, u32[]{:S(2)}) copy-start(f32[32,4096]{1,0:T(8,128)} %reduce-scatter.5.cloned.1.call-done) | copy-start | bytes 1572868
Sparse Core Ops, SparseCore 0:
  9.9 30.4 all-gather.1
  61.2 51.0 reduce-scatter.6
  114.6 43.6 reduce-scatter.4
